TPU v7x, 512 devices: a whole 4x8x8 slice. The times are simulated.
512 devices in a mesh: expert: 32 (over z, y_hi), tensor: 16 (over y_lo, x, core).
Axes of the slice: x: 4, y: 8 (y_hi: 4, y_lo: 2; y = y_hi * 2 + y_lo), z: 8, core: 2. Of those that a mesh axis runs over, the one named last changes fastest.
Arguments:
- tokens: bfloat16 [4096, 3072], P('expert', 'tensor'), may hold values from -6 to 6
- expert_ids: int32 [4096, 2], P('expert'), may hold values from 0 to 7, all different within a row; in each aligned block of 128 rows (0 to 127, 128 to 255, ...) at most 48 rows name the same one
- joined_weight: bfloat16 [32, 3072, 2, 4096], P('expert', 'tensor'), may hold values from -0.109375 to 0.109375
Outputs:
- hidden: bfloat16 [4096, 2, 4, 4096], P('expert', None, None, 'tensor')
Inputs may be any that keep to these rules, and one draw needn't show every extreme that they name: `expert_ids`: each row names 2 different experts. Among the rows of one device (each aligned block of 128 rows) no expert is named by more than 48 rows, and in some blocks one expert is named by exactly 48 rows.
All inputs are finite; a program needn't handle non-finite values.
Results may differ from a plain program's by a relative error of at most 0.001.
Values may be sent and summed in bfloat16 or wider, within the bound.
No kernel may reach another device: no remote copies, remote signals or barrier semaphores. Data moves between devices by JAX's collectives and lax.ppermute only.
A program may use at most 128 MiB of HBM per device.

v0:
```python
import jax
import jax.numpy as jnp
from jax import lax
from jax.sharding import PartitionSpec as P

E = 8
TOP = 2
CAP = 48


def activate(gate_up, half_width):
    gate = gate_up[:, :half_width]
    upward = gate_up[:, half_width:]
    return (jax.nn.silu(gate) * upward).astype(jnp.bfloat16)


def give_back(active):
    return lax.all_to_all(active, "expert", split_axis=0, concat_axis=0, tiled=True)


def local(tokens, expert_ids, joined_weight):
    groups = lax.axis_size("tensor")
    blocks = lax.axis_size("expert")
    copies = blocks // E
    local_rows = joined_weight.shape[1]
    half_width = joined_weight.shape[3] // groups
    pieces = joined_weight[0].reshape(local_rows, 2, groups, half_width)
    arranged = lax.all_to_all(pieces, "tensor", split_axis=2, concat_axis=0, tiled=True)
    weights = arranged.reshape(local_rows * groups, 2 * half_width)
    tok_count = tokens.shape[0]
    flat_ids = expert_ids.reshape(-1)
    chosen = (flat_ids[:, None] == jnp.arange(E, dtype=jnp.int32)[None, :]).astype(jnp.int32)
    earlier = jnp.cumsum(chosen, axis=0) - chosen
    position = jnp.sum(earlier * chosen, axis=1)
    slot_index = flat_ids * CAP + position
    pick_table = (slot_index[:, None] == jnp.arange(E * CAP, dtype=jnp.int32)[None, :]).astype(
        jnp.bfloat16
    )
    token_table = pick_table.reshape(tok_count, TOP, E * CAP).sum(axis=1)
    width = tokens.shape[1]
    placed = lax.dot_general(
        token_table, tokens, (((0,), (0,)), ((), ())), preferred_element_type=jnp.float32
    )
    placed = placed.astype(jnp.bfloat16).reshape(E, 1, CAP, width)
    outgoing = jnp.broadcast_to(placed, (E, copies, CAP, width)).reshape(blocks, CAP, width)
    received = lax.all_to_all(outgoing, "expert", split_axis=0, concat_axis=0, tiled=True)
    slot_count = received.shape[1]
    piece = lax.all_gather(received, "tensor", axis=2, tiled=True)
    row_block = piece.reshape(blocks * slot_count, piece.shape[2])
    gate_up = jnp.dot(row_block, weights, preferred_element_type=jnp.float32)
    returned = give_back(activate(gate_up, half_width).reshape(blocks, slot_count, half_width))
    grouped = (
        returned.reshape(E, copies, CAP, half_width)
        .transpose(0, 2, 1, 3)
        .reshape(E * CAP, copies * half_width)
    )
    hidden = jnp.dot(pick_table, grouped, preferred_element_type=jnp.float32).astype(jnp.bfloat16)
    return hidden.reshape(tok_count, TOP, copies, half_width)


def solution(mesh):
    placed = (P("expert", "tensor"), P("expert", None), P("expert", "tensor", None, None))
    return jax.shard_map(
        local,
        mesh=mesh,
        in_specs=placed,
        out_specs=P("expert", None, None, "tensor"),
        check_vma=False,
    )
```

profile of v0, /device:TPU:10, one launch (start us, length us, event | category | flops | bytes accessed | tf_op | source)
XLA Modules:
  0.0 299.9 jit_solution(4116273108823073041)
XLA Ops:
  6.5 0.0 all-gather.2.cloned.1.call-start
  6.5 0.8 copy.55
  7.3 0.1 reshape.62
  7.5 0.1 eq.46
  7.6 0.6 reduce-window.6
  8.2 0.2 slice_reduce_fusion
  8.5 0.1 fusion.5
  8.6 0.1 reduce_sum.24
  8.7 0.1 copy.57
  8.8 0.7 multiply_add_fusion
  9.5 0.1 fusion.2
  9.6 0.0 copy-done
  9.6 0.2 convolution_convert_fusion.1
  9.8 0.1 copy.58
  9.9 0.1 broadcast_in_dim.5
  10.0 37.4 %all_to_all.25 = bf16[32,48,192]{2,1,0:T(8,128)(2,1)S(1)} all-to-all(bf16[32,48,192]{2,1,0:T(8,128)(2,1)S(1)} %bitcast.36), channel_id=1, replica_groups=mesh['expert'=32,'tensor'=16] {'expert'}, dimensions={0} | all-to-all | bytes 1179648 | tf_op jit(solution)/shard_map/all_to_all | solution.py:46
  47.4 2.3 copy.59
  49.7 0.0 all-gather.2.cloned.1.call-update
  49.7 4.6 %reshape_squeeze.3 = bf16[192,2,16,256]{3,2,1,0:T(8,128)(2,1)S(1)} reshape(bf16[1,192,2,4096]{3,2,1,0:T(2,128)(2,1)} %param.5) | data formatting | bytes 6291456 | tf_op jit(solution)/shard_map/reshape;squeeze | solution.py:27
  54.3 3.0 %copy.61 = bf16[192,2,16,256]{3,1,0,2:T(2,128)(2,1)S(1)} copy(bf16[192,2,16,256]{3,2,1,0:T(8,128)(2,1)S(1)} %reshape_squeeze.3) | data formatting | bytes 6291456 | tf_op jit(solution)/shard_map/reshape;squeeze | solution.py:27
  57.3 75.2 %all_to_all.26 = bf16[192,2,16,256]{3,1,0,2:T(2,128)(2,1)S(1)} all-to-all(bf16[192,2,16,256]{3,1,0,2:T(2,128)(2,1)S(1)} %copy.61), channel_id=1, replica_groups=mesh['expert'=32,'tensor'=16] {'tensor'}, dimensions={2} | all-to-all | bytes 6291456 | tf_op jit(solution)/shard_map/all_to_all | solution.py:28
  132.5 0.5 copy.63
  133.1 86.2 %all-gather.2.cloned.1.call-done = bf16[32,48,3072]{1,0,2:T(8,128)(2,1)} async-done(((bf16[32,48,192]{1,0,2:T(8,128)(2,1)}), bf16[32,48,3072]{1,0,2:T(8,128)(2,1)}) %all-gather.2.cloned.1.call-update) | async-done | bytes 9437200 | tf_op jit(solution)/shard_map/all_gather | solution.py:48
  219.3 26.3 %copy.60 = bf16[32,48,3072]{2,1,0:T(8,128)(2,1)} copy(bf16[32,48,3072]{1,0,2:T(8,128)(2,1)} %all-gather.2.cloned.1.call-done) | data formatting | bytes 18874368 | tf_op jit(solution)/shard_map/all_gather | solution.py:48
  245.5 7.5 %fusion.7 = f32[1536,512]{1,0:T(8,128)S(1)} fusion(bf16[1536,3072]{1,0:T(8,128)(2,1)} %bitcast.31, bf16[3072,512]{1,0:T(8,128)(2,1)S(1)} %bitcast.32), kind=kOutput, calls=%fused_computation.18 | convolution fusion | flops 4831838208 | bytes 15728640 | tf_op jit(solution)/shard_map/dot_general | solution.py:50
  253.1 1.3 fusion
  254.4 9.7 %all-to-all-start.2 = ((bf16[32,48,256]{2,1,0:T(8,128)(2,1)}), bf16[32,48,256]{2,1,0:T(8,128)(2,1)S(1)}, u32[]{:S(2)}, u32[]{:S(2)}) async-start(bf16[32,48,256]{2,1,0:T(8,128)(2,1)} %bitcast.7), calls=%async_computation.2 | async-start | bytes 1572864 | tf_op jit(solution)/shard_map/all_to_all | solution.py:18
  264.1 26.8 %all-to-all-done.2 = bf16[32,48,256]{2,1,0:T(8,128)(2,1)S(1)} async-done(((bf16[32,48,256]{2,1,0:T(8,128)(2,1)}), bf16[32,48,256]{2,1,0:T(8,128)(2,1)S(1)}, u32[]{:S(2)}, u32[]{:S(2)}) %all-to-all-start.2) | async-done | bytes 786464 | tf_op jit(solution)/shard_map/all_to_all | solution.py:18
  290.8 0.4 copy.62
  291.3 0.2 copy.64
  291.4 0.5 convolution_convert_fusion
  291.9 1.2 reshape.70
  (5 shorter events, 0.1 us)
Async XLA Ops:
  6.5 3.1 %copy-start = (bf16[128,192]{0,1:T(8,128)(2,1)S(1)}, bf16[128,192]{0,1:T(8,128)(2,1)}, u32[]{:S(2)}) copy-start(bf16[128,192]{0,1:T(8,128)(2,1)} %param.3) | copy-start | bytes 147460
  6.5 212.7 %all-gather.2.cloned.1.call-start = ((), (), s32[]{:S(2)}) async-start(), calls=%async_computation.3 | async-start | bytes 26738688 | tf_op jit(solution)/shard_map/all_gather | solution.py:48
  254.4 36.5 %all-to-all-start.2 = ((bf16[32,48,256]{2,1,0:T(8,128)(2,1)}), bf16[32,48,256]{2,1,0:T(8,128)(2,1)S(1)}, u32[]{:S(2)}, u32[]{:S(2)}) async-start(bf16[32,48,256]{2,1,0:T(8,128)(2,1)} %bitcast.7), calls=%async_computation.2 | async-start | bytes 1572864 | tf_op jit(solution)/shard_map/all_to_all | solution.py:18
Sparse Core Ops, SparseCore 0:
  49.8 169.3 all-gather.1
where the time goes:
time: 301 us; the launch traced here: 300 us
  blocking collectives  113 us (38%)
  waiting for transfers between devices  113 us (38%)
  local copies, waits for them, and re-layouts  40.1 us (13%)
  between operations  13.5 us (4%)
  starting transfers between devices  9.68 us (3%)
  matrix products  8.2 us (3%)
    all_gather x1, waiting for transfers between devices, local(): piece = lax.all_gather(received, 'tensor', axis=2, tiled=True)  86.2 us
    all_to_all x1, blocking collectives, local(): lax.all_to_all(pieces, 'tensor', split_axis=2, concat_axis=0, tiled=True)  75.2 us
    all_to_all x1, blocking collectives, local(): lax.all_to_all(outgoing, 'expert', split_axis=0, concat_axis=0, tiled=True)  37.4 us
    all_to_all x1, waiting for transfers between devices, give_back(): lax.all_to_all(active, 'expert', split_axis=0, concat_axis=0, tiled=True)  26.8 us
    all_gather x1, local copies, waits for them, and re-layouts, local(): piece = lax.all_gather(received, 'tensor', axis=2, tiled=True)  26.3 us
    all_to_all x1, starting transfers between devices, give_back(): lax.all_to_all(active, 'expert', split_axis=0, concat_axis=0, tiled=True)  9.68 us
    another operation x2, local copies, waits for them, and re-layouts, local(): pieces = joined_weight[0].reshape(local_rows, 2, groups, half_width)  7.59 us
    dot_general x1, matrix products, local(): gate_up = jnp.dot(row_block, weights, preferred_element_type=jnp.float32)  7.53 us
  transfers between devices with their start and end apart: 2, of which 2 were waited for; matrix products, arithmetic and copies ran while one was open for 3% of the time, Pallas kernels for 0%

commit v1 on v0

--- a/solution.py
+++ b/solution.py
@@ -1,11 +1,22 @@
+import functools
 import jax
 import jax.numpy as jnp
 from jax import lax
 from jax.sharding import PartitionSpec as P
+from jax.lax import all_to_all, psum
 
 E = 8
 TOP = 2
 CAP = 48
+
+
+def groups_push(matrix, on_dim):
+    return jnp.concatenate(
+        all_to_all(jnp.stack(psum(1, "tensor") * [matrix], axis=0), "tensor", 0, 0), on_dim
+    )
+
+
+form_series_all = functools.partial(groups_push, on_dim=2)
 
 
 def activate(gate_up, half_width):
@@ -45,7 +56,7 @@
     outgoing = jnp.broadcast_to(placed, (E, copies, CAP, width)).reshape(blocks, CAP, width)
     received = lax.all_to_all(outgoing, "expert", split_axis=0, concat_axis=0, tiled=True)
     slot_count = received.shape[1]
-    piece = lax.all_gather(received, "tensor", axis=2, tiled=True)
+    piece = form_series_all(received)
     row_block = piece.reshape(blocks * slot_count, piece.shape[2])
     gate_up = jnp.dot(row_block, weights, preferred_element_type=jnp.float32)
     returned = give_back(activate(gate_up, half_width).reshape(blocks, slot_count, half_width))

time: 301 us -> 376 us (1.25)
  the two profiles are of different devices: /device:TPU:10 before, /device:TPU:14 now
where the time goes in v1:
time: 376 us; the launch traced here: 375 us
  waiting for transfers between devices  232 us (62%)
  local copies, waits for them, and re-layouts  57 us (15%)
  blocking collectives  45 us (12%)
  starting transfers between devices  29.3 us (8%)
  matrix products  8.22 us (2%)
    all_to_all x1, waiting for transfers between devices, groups_push(): all_to_all(jnp.stack(psum(1, 'tensor') * [matrix], axis=0), 'tensor', 0, 0)  192 us
    all_to_all x1, blocking collectives, local(): lax.all_to_all(pieces, 'tensor', split_axis=2, concat_axis=0, tiled=True)  45 us
    all_to_all x1, waiting for transfers between devices, give_back(): lax.all_to_all(active, 'expert', split_axis=0, concat_axis=0, tiled=True)  26.8 us
    another operation x1, local copies, waits for them, and re-layouts, local(): row_block = piece.reshape(blocks * slot_count, piece.shape[2])  20.4 us
    all_to_all x1, starting transfers between devices, local(): lax.all_to_all(outgoing, 'expert', split_axis=0, concat_axis=0, tiled=True)  15.2 us
    reshape x1, local copies, waits for them, and re-layouts, groups_push(): jnp.concatenate(all_to_all(jnp.stack(psum(1, 'tensor') * [matrix], axis=0...  14.1 us
    all_to_all x1, waiting for transfers between devices, local(): lax.all_to_all(outgoing, 'expert', split_axis=0, concat_axis=0, tiled=True)  13.4 us
    another operation x2, local copies, waits for them, and re-layouts, local(): pieces = joined_weight[0].reshape(local_rows, 2, groups, half_width)  9.07 us
  transfers between devices with their start and end apart: 3, of which 3 were waited for; matrix products, arithmetic and copies ran while one was open for 3% of the time, Pallas kernels for 0%

profile of v1, /device:TPU:14, one launch (start us, length us, event | category | flops | bytes accessed | tf_op | source)
XLA Modules:
  0.0 374.8 jit_solution(14164862038640929089)
XLA Ops:
  0.0 0.8 copy.36
  0.8 0.1 eq.46
  0.9 0.1 reshape.64
  1.1 0.6 reduce-window.6
  1.7 0.2 slice_reduce_fusion
  1.9 0.1 fusion.5
  2.0 0.1 reduce_sum.24
  2.2 0.1 copy.38
  2.2 0.7 multiply_add_fusion
  2.9 0.1 fusion.2
  3.1 0.2 convolution_convert_fusion.1
  3.3 0.1 copy.39
  3.4 0.9 broadcast_in_dim.5
  4.3 15.2 %all-to-all-start = ((bf16[32,48,192]{2,1,0:T(8,128)(2,1)}), bf16[32,48,192]{2,1,0:T(8,128)(2,1)}, u32[]{:S(2)}, u32[]{:S(2)}) async-start(bf16[32,48,192]{2,1,0:T(8,128)(2,1)} %bitcast.3), calls=%async_computation | async-start | bytes 1572864 | tf_op jit(solution)/shard_map/all_to_all | solution.py:57
  19.5 4.6 %reshape_squeeze.3 = bf16[192,2,16,256]{3,2,1,0:T(8,128)(2,1)S(1)} reshape(bf16[1,192,2,4096]{3,2,1,0:T(2,128)(2,1)} %param.5) | data formatting | bytes 6291456 | tf_op jit(solution)/shard_map/reshape;squeeze | solution.py:38
  24.1 4.5 %copy.41 = bf16[192,2,16,256]{3,1,0,2:T(2,128)(2,1)} copy(bf16[192,2,16,256]{3,2,1,0:T(8,128)(2,1)S(1)} %reshape_squeeze.3) | data formatting | bytes 6291456 | tf_op jit(solution)/shard_map/reshape;squeeze | solution.py:38
  28.6 13.4 %all-to-all-done = bf16[32,48,192]{2,1,0:T(8,128)(2,1)} async-done(((bf16[32,48,192]{2,1,0:T(8,128)(2,1)}), bf16[32,48,192]{2,1,0:T(8,128)(2,1)}, u32[]{:S(2)}, u32[]{:S(2)}) %all-to-all-start) | async-done | bytes 589856 | tf_op jit(solution)/shard_map/all_to_all | solution.py:57
  42.0 45.0 %all_to_all.30 = bf16[192,2,16,256]{3,1,0,2:T(2,128)(2,1)S(1)} all-to-all(bf16[192,2,16,256]{3,1,0,2:T(2,128)(2,1)} %copy.41), channel_id=1, replica_groups=mesh['expert'=32,'tensor'=16] {'tensor'}, dimensions={2} | all-to-all | bytes 6291456 | tf_op jit(solution)/shard_map/all_to_all | solution.py:39
  87.0 6.8 %stack.2 = bf16[16,32,48,192]{3,2,1,0:T(8,128)(2,1)} broadcast(bf16[32,48,192]{2,1,0:T(8,128)(2,1)} %all-to-all-done), dimensions={1,2,3} | broadcast | bytes 10027008 | tf_op jit(solution)/shard_map/stack | solution.py:15
  93.8 7.7 %all-to-all-start.1 = ((bf16[16,32,48,192]{3,2,1,0:T(8,128)(2,1)}), bf16[16,32,48,192]{3,2,1,0:T(8,128)(2,1)}, u32[]{:S(2)}, u32[]{:S(2)}) async-start(bf16[16,32,48,192]{3,2,1,0:T(8,128)(2,1)} %stack.2), calls=%async_computation.1 | async-start | bytes 25165824 | tf_op jit(solution)/shard_map/all_to_all | solution.py:15
  101.6 2.3 copy.43
  103.9 192.0 %all-to-all-done.1 = bf16[16,32,48,192]{3,2,1,0:T(8,128)(2,1)} async-done(((bf16[16,32,48,192]{3,2,1,0:T(8,128)(2,1)}), bf16[16,32,48,192]{3,2,1,0:T(8,128)(2,1)}, u32[]{:S(2)}, u32[]{:S(2)}) %all-to-all-start.1) | async-done | bytes 9437216 | tf_op jit(solution)/shard_map/all_to_all | solution.py:15
  295.9 14.1 %copy.40 = bf16[32,48,16,192]{3,2,1,0:T(8,128)(2,1)} copy(bf16[32,48,16,192]{3,1,0,2:T(8,128)(2,1)} %bitcast.4) | data formatting | bytes 18874368 | tf_op jit(solution)/shard_map/reshape | solution.py:14
  310.0 20.4 %reshape_reshape.3 = bf16[1536,3072]{1,0:T(8,128)(2,1)} reshape(bf16[32,48,16,192]{3,2,1,0:T(8,128)(2,1)} %copy.40) | data formatting | bytes 18874368 | tf_op jit(solution)/shard_map/reshape;reshape | solution.py:60
  330.3 7.5 %fusion.7 = f32[1536,512]{1,0:T(8,128)S(1)} fusion(bf16[1536,3072]{1,0:T(8,128)(2,1)} %reshape_reshape.3, bf16[3072,512]{1,0:T(8,128)(2,1)S(1)} %bitcast.33), kind=kOutput, calls=%fused_computation.18 | convolution fusion | flops 4831838208 | bytes 15728640 | tf_op jit(solution)/shard_map/dot_general | solution.py:61
  337.9 1.3 fusion
  339.2 6.4 %all-to-all-start.3 = ((bf16[32,48,256]{2,1,0:T(8,128)(2,1)}), bf16[32,48,256]{2,1,0:T(8,128)(2,1)S(1)}, u32[]{:S(2)}, u32[]{:S(2)}) async-start(bf16[32,48,256]{2,1,0:T(8,128)(2,1)} %bitcast.7), calls=%async_computation.3 | async-start | bytes 1572864 | tf_op jit(solution)/shard_map/all_to_all | solution.py:29
  345.7 26.8 %all-to-all-done.3 = bf16[32,48,256]{2,1,0:T(8,128)(2,1)S(1)} async-done(((bf16[32,48,256]{2,1,0:T(8,128)(2,1)}), bf16[32,48,256]{2,1,0:T(8,128)(2,1)S(1)}, u32[]{:S(2)}, u32[]{:S(2)}) %all-to-all-start.3) | async-done | bytes 786464 | tf_op jit(solution)/shard_map/all_to_all | solution.py:29
  372.5 0.4 copy.42
  373.0 0.2 copy.44
  373.1 0.5 convolution_convert_fusion
  373.6 1.2 reshape.72
  (10 shorter events, 0.1 us)
Async XLA Ops:
  0.0 3.1 copy-start
  4.3 37.7 %all-to-all-start = ((bf16[32,48,192]{2,1,0:T(8,128)(2,1)}), bf16[32,48,192]{2,1,0:T(8,128)(2,1)}, u32[]{:S(2)}, u32[]{:S(2)}) async-start(bf16[32,48,192]{2,1,0:T(8,128)(2,1)} %bitcast.3), calls=%async_computation | async-start | bytes 1572864 | tf_op jit(solution)/shard_map/all_to_all | solution.py:57
  93.8 202.0 %all-to-all-start.1 = ((bf16[16,32,48,192]{3,2,1,0:T(8,128)(2,1)}), bf16[16,32,48,192]{3,2,1,0:T(8,128)(2,1)}, u32[]{:S(2)}, u32[]{:S(2)}) async-start(bf16[16,32,48,192]{3,2,1,0:T(8,128)(2,1)} %stack.2), calls=%async_computation.1 | async-start | bytes 25165824 | tf_op jit(solution)/shard_map/all_to_all | solution.py:15
  310.0 20.4 %copy-start.2 = (bf16[384,8,2,256]{3,1,2,0:T(8,128)(2,1)S(1)}, bf16[384,8,2,256]{3,1,2,0:T(8,128)(2,1)}, u32[]{:S(2)}) copy-start(bf16[384,8,2,256]{3,1,2,0:T(8,128)(2,1)} %copy.43) | copy-start | bytes 9437188
  339.2 33.3 %all-to-all-start.3 = ((bf16[32,48,256]{2,1,0:T(8,128)(2,1)}), bf16[32,48,256]{2,1,0:T(8,128)(2,1)S(1)}, u32[]{:S(2)}, u32[]{:S(2)}) async-start(bf16[32,48,256]{2,1,0:T(8,128)(2,1)} %bitcast.7), calls=%async_computation.3 | async-start | bytes 1572864 | tf_op jit(solution)/shard_map/all_to_all | solution.py:29
  345.7 29.1 %copy-start.1 = (bf16[128,192]{0,1:T(8,128)(2,1)S(1)}, bf16[128,192]{0,1:T(8,128)(2,1)}, u32[]{:S(2)}) copy-start(bf16[128,192]{0,1:T(8,128)(2,1)} %param.3) | copy-start | bytes 147460
